TPU v7x, 32 devices: a whole 2x2x4 slice. The times are simulated.
32 devices in a mesh: row: 8 (over y, x, core), col: 4 (over z).
Axes of the slice: x: 2, y: 2, z: 4, core: 2. Of those that a mesh axis runs over, the one named last changes fastest.
Arguments:
- expression: bfloat16 [4096, 1024], P(('row', 'col')), may hold values from -200 to 200, as said below
- powers: int32 [10], replicated, may hold values from 1 to 20
Outputs:
- log_degree: float32 [10, 4096], P(None, ('row', 'col'))
- degree_freq: float32 [10, 10], replicated
- fit_slope: float32 [10], replicated
- mean_log: float32 [10], replicated
Inputs may be any that keep to these rules, and one draw needn't show every extreme that they name: Finite expression values.
All inputs are finite; a program needn't handle non-finite values.
Results may differ from a plain program's by a relative error of at most 0.0003.
Values may be sent and summed in bfloat16 or wider, within the bound.
A program may use at most 64 MiB of HBM per device.

v0:
```python
import jax
import jax.numpy as jnp
from jax import lax
from jax.sharding import PartitionSpec as P

BINS = 10


def gene_stats(genes):
    values = genes.astype(jnp.float32)
    gene_mean = jnp.mean(values, axis=1)
    centred = values - gene_mean[:, None]
    gene_inv = lax.rsqrt(jnp.mean(centred * centred, axis=1) + 1e-06)
    return (gene_mean, gene_inv)


def add_slice(totals, addend, start):
    current = lax.dynamic_slice_in_dim(totals, start, addend.shape[1], 1)
    return lax.dynamic_update_slice_in_dim(totals, current + addend, start, 1)


def block_sums(left_genes, right_genes, exponents, row_list, carry, left_start):
    row_count = left_genes.shape[0]
    block_rows = 256
    samples = left_genes.shape[1]
    left_mean, left_inv = gene_stats(left_genes)
    right_mean, right_inv = gene_stats(right_genes)

    def one_block(block_index, totals):
        row_totals, column_totals = totals
        offset = block_index * block_rows
        row_block = lax.dynamic_slice_in_dim(left_genes, offset, block_rows, 0)
        block_mean = lax.dynamic_slice_in_dim(left_mean, offset, block_rows, 0)
        block_inv = lax.dynamic_slice_in_dim(left_inv, offset, block_rows, 0)
        raw = lax.dot_general(
            row_block, right_genes, (((1,), (1,)), ((), ())), preferred_element_type=jnp.float32
        )
        pearson = (
            (raw / samples - block_mean[:, None] * right_mean[None, :])
            * block_inv[:, None]
            * right_inv[None, :]
        )
        log_abs = jnp.log(jnp.abs(pearson))
        row_parts = []
        for power_index in row_list:
            row_parts.append(jnp.sum(jnp.exp(exponents[power_index] * log_abs), axis=1))
        if row_parts:
            row_totals = add_slice(row_totals, jnp.stack(row_parts), left_start + offset)
        return (row_totals, column_totals)

    return lax.fori_loop(0, row_count // block_rows, one_block, carry)


def on_device(expression, powers):
    exponents = powers.astype(jnp.float32)
    npower = powers.shape[0]
    local_genes = expression.shape[0]
    row_width = local_genes * lax.axis_size("col")
    column_width = local_genes * lax.axis_size("row")
    row_list = list(range(npower))
    col_list = []
    initial = (
        jnp.zeros((len(row_list), row_width), jnp.float32),
        jnp.zeros((max(len(col_list), 1), column_width), jnp.float32),
    )
    left_genes = lax.all_gather(expression, "col", axis=0, tiled=True)
    row_totals, column_totals = block_sums(
        left_genes,
        lax.all_gather(expression, "row", axis=0, tiled=True),
        exponents,
        row_list,
        initial,
        0,
    )
    degree = lax.psum_scatter(row_totals, "col", scatter_dimension=1, tiled=True)
    peak = lax.pmax(jnp.max(degree, axis=1), ("row", "col"))
    position = jnp.clip(BINS * degree / peak[:, None] - 0.5, 0.0, BINS - 1.0)
    centres = jnp.arange(BINS, dtype=jnp.float32)
    weights = jnp.maximum(0.0, 1.0 - jnp.abs(position[:, :, None] - centres[None, None, :]))
    freq_total, degree_total = lax.psum(
        (jnp.sum(weights, axis=1), jnp.sum(degree, axis=1)), ("row", "col")
    )
    genes_all = local_genes * lax.axis_size("row") * lax.axis_size("col")
    degree_freq = freq_total / genes_all
    mean_log = jnp.log10(degree_total / genes_all)
    xfit = jnp.log10((centres[None, :] + 0.5) * peak[:, None] / BINS)
    yfit = jnp.log10(degree_freq + 1.0 / genes_all)
    xdev = xfit - jnp.mean(xfit, axis=1, keepdims=True)
    ydev = yfit - jnp.mean(yfit, axis=1, keepdims=True)
    fit_slope = jnp.sum(xdev * ydev, axis=1) / jnp.sum(xdev * xdev, axis=1)
    return (jnp.log10(degree), degree_freq, fit_slope, mean_log)


def solution(mesh):
    return jax.shard_map(
        on_device,
        mesh=mesh,
        in_specs=(P(("row", "col"), None), P()),
        out_specs=(P(None, ("row", "col")), P(), P(), P()),
        check_vma=False,
    )
```

profile of v0, /device:TPU:0, one launch (start us, length us, event | category | flops | bytes accessed | tf_op | source)
XLA Modules:
  0.0 201.4 jit_solution(1471055572352535315)
XLA Ops:
  7.2 0.0 all-gather.3.cloned.1.call-start
  7.2 0.7 all-gather.3.cloned.1.call-update
  7.9 0.0 all-gather.5.cloned.1.call-start
  7.9 0.7 all-gather.5.cloned.1.call-update
  8.6 0.0 reduce-scatter.2.cloned.1.call-start
  8.7 0.7 convert_element_type.9
  9.4 30.9 %all-gather.3.cloned.1.call-done = bf16[512,1024]{1,0:T(8,128)(2,1)} async-done(((bf16[128,1024]{1,0:T(8,128)(2,1)}), bf16[512,1024]{1,0:T(8,128)(2,1)}) %all-gather.3.cloned.1.call-update) | async-done | bytes 1048592 | tf_op jit(solution)/shard_map/all_gather | solution.py:66
  40.3 1.4 convert_reduce_fusion.1
  41.7 1.6 fusion.10
  43.4 26.0 %all-gather.5.cloned.1.call-done = bf16[1024,1024]{1,0:T(8,128)(2,1)} async-done(((bf16[128,1024]{1,0:T(8,128)(2,1)}), bf16[1024,1024]{1,0:T(8,128)(2,1)}) %all-gather.5.cloned.1.call-update) | async-done | bytes 2097168 | tf_op jit(solution)/shard_map/all_gather | solution.py:69
  69.4 0.0 copy-start
  69.4 0.0 copy-start.1
  69.4 2.1 %convert_reduce_fusion = f32[1024]{0:T(1024)S(1)} fusion(bf16[1024,1024]{1,0:T(8,128)(2,1)} %all-gather.5.cloned.1.call-done), kind=kLoop, calls=%fused_computation.20 | loop fusion | flops 2096128 | bytes 2101248 | tf_op jit(solution)/shard_map/reduce_sum | solution.py:11
  71.5 0.1 copy-done
  71.6 0.7 fusion.8
  72.3 0.0 copy-done.1
  72.3 19.4 %while.13 = (s32[]{:T(128)}, f32[10,512]{1,0:T(8,128)S(1)}, f32[10]{0:T(128)S(1)}, bf16[512,1024]{1,0:T(8,128)(2,1)S(1)}, bf16[1024,1024]{1,0:T(8,128)(2,1)S(1)}...) while((s32[]{:T(128)}, f32[10,512]{1,0:T(8,128)S(1)}, ...), condition=%wide.region_15.0_spmd, body=%wide.region_4.0_spmd.sunk | while | flops 543686656 | bytes 2715955 | solution.py:51
  72.3 0.1 dynamic_slice.39
  72.4 0.1 dynamic_slice.40
  72.5 0.7 fusion.20
  73.2 8.8 %exponential_reduce_fusion.11 = (f32[256]{0:T(256)S(1)}, f32[256]{0:T(256)S(1)}, f32[256]{0:T(256)S(1)}, f32[256]{0:T(256)S(1)}, f32[256]{0:T(256)S(1)}, /*index...) fusion(f32[]{:T(128)} %bitcast.43, f32[]{:T(128)} %bitcast.44, ...), kind=kOutput, calls=%fused_computation.6.clone.1 | convolution fusion | flops 543684096 | bytes 2641964 | tf_op jit(solution)/shard_map/while/body/eval_jaxpr/dot_general | solution.py:35
  81.9 0.1 stack.78
  82.0 0.1 dynamic_slice.39
  82.1 0.1 dynamic_slice.40
  82.2 0.7 fusion.20
  82.9 8.8 %exponential_reduce_fusion.11 = (f32[256]{0:T(256)S(1)}, f32[256]{0:T(256)S(1)}, f32[256]{0:T(256)S(1)}, f32[256]{0:T(256)S(1)}, f32[256]{0:T(256)S(1)}, /*index...) fusion(f32[]{:T(128)} %bitcast.43, f32[]{:T(128)} %bitcast.44, ...), kind=kOutput, calls=%fused_computation.6.clone.1 | convolution fusion | flops 543684096 | bytes 2641964 | tf_op jit(solution)/shard_map/while/body/eval_jaxpr/dot_general | solution.py:35
  91.6 0.1 stack.78
  91.7 0.0 copy-start.2
  91.7 0.6 copy-done.2
  92.3 0.0 reduce-scatter.2.cloned.1.call-update
  92.4 19.3 %reduce-scatter.2.cloned.1.call-done = f32[10,128]{1,0:T(8,128)} async-done(((f32[10,512]{1,0:T(8,128)}), f32[10,128]{1,0:T(8,128)}) %reduce-scatter.2.cloned.1.call-update) | async-done | bytes 5136 | tf_op jit(solution)/shard_map/reduce_scatter | solution.py:75
  111.7 0.8 fusion.14
  112.5 38.4 %pmax.7 = f32[10]{0:T(128)S(1)} all-reduce(f32[10]{0:T(128)S(1)} %get-tuple-element.170), channel_id=1, replica_groups=mesh['row'=8,'col'=4] {'row','col'}, use_global_device_ids=true, to_apply=%region_18.0 | all-reduce | flops 10 | bytes 80 | tf_op jit(solution)/shard_map/pmax | solution.py:76
  150.9 1.3 add_clamp_fusion
  152.2 0.1 maximum_reduce_fusion
  152.3 40.9 %all-reduce = (f32[10,10]{1,0:T(8,128)S(1)}, f32[10]{0:T(128)S(1)}) all-reduce(f32[10,10]{1,0:T(8,128)S(1)} %maximum_reduce_fusion, f32[10]{0:T(128)S(1)} %get-tuple-element.169), channel_id=1, replica_groups=mesh['row'=8,'col'=4] {'row','col'}, use_global_device_ids=true, to_apply=%region_20.21 | all-reduce | flops 110 | bytes 880 | tf_op jit(solution)/shard_map/psum | solution.py:80
  193.3 0.1 fusion.13
  193.4 0.0 copy-start.3
  193.4 0.2 fusion.12
  193.6 0.5 log_multiply_fusion.3
  194.1 0.2 multiply_reduce_fusion
  194.3 0.5 div.61
  194.9 0.0 copy-done.3
  (10 shorter events, 0.1 us)
Async XLA Ops:
  7.2 33.1 %all-gather.3.cloned.1.call-start = ((), (), s32[]{:S(2)}) async-start(), calls=%async_computation.1 | async-start | bytes 1310720 | tf_op jit(solution)/shard_map/all_gather | solution.py:66
  7.9 61.5 %all-gather.5.cloned.1.call-start = ((), (), s32[]{:S(2)}) async-start(), calls=%async_computation.2 | async-start | bytes 2359296 | tf_op jit(solution)/shard_map/all_gather | solution.py:69
  8.6 103.0 %reduce-scatter.2.cloned.1.call-start = ((), (), s32[]{:S(2)}) async-start(), calls=%async_computation.3 | async-start | bytes 40960 | tf_op jit(solution)/shard_map/reduce_scatter | solution.py:75
  69.4 2.2 %copy-start = (bf16[1024,1024]{1,0:T(8,128)(2,1)S(1)}, bf16[1024,1024]{1,0:T(8,128)(2,1)}, u32[]{:S(2)}) copy-start(bf16[1024,1024]{1,0:T(8,128)(2,1)} %all-gather.5.cloned.1.call-done) | copy-start | bytes 6291460
  69.4 2.9 %copy-start.1 = (bf16[512,1024]{1,0:T(8,128)(2,1)S(1)}, bf16[512,1024]{1,0:T(8,128)(2,1)}, u32[]{:S(2)}) copy-start(bf16[512,1024]{1,0:T(8,128)(2,1)} %all-gather.3.cloned.1.call-done) | copy-start | bytes 3145732
  91.7 0.6 copy-start.2
  193.4 1.5 copy-start.3
Sparse Core Ops, SparseCore 0:
  9.5 30.6 all-gather.2
  42.2 27.1 all-gather.4
  92.5 19.1 reduce-scatter.1
where the time goes:
time: 202 us; the launch traced here: 201 us
  blocking collectives  79.4 us (39%)
  waiting for transfers between devices  77.6 us (38%)
  matrix products  17.6 us (9%)
  between operations  13.8 us (7%)
  other arithmetic  10.3 us (5%)
  local copies, waits for them, and re-layouts  2.49 us (1%)
    psum x1, blocking collectives, on_device(): lax.psum((jnp.sum(weights, axis=1), jnp.sum(degree, axis=1)), ('row', 'co...  40.9 us
    pmax x1, blocking collectives, on_device(): peak = lax.pmax(jnp.max(degree, axis=1), ('row', 'col'))  38.4 us
    all_gather x1, waiting for transfers between devices, on_device(): left_genes = lax.all_gather(expression, 'col', axis=0, tiled=True)  30.9 us
    all_gather x1, waiting for transfers between devices, on_device(): lax.all_gather(expression, 'row', axis=0, tiled=True)  26 us
    reduce_scatter x1, waiting for transfers between devices, on_device(): lax.psum_scatter(row_totals, 'col', scatter_dimension=1, tiled=True)  19.3 us
    dot_general x2, matrix products, one_block(): lax.dot_general(row_block, right_genes, (((1,), (1,)), ((), ())), preferr...  17.6 us
  transfers between devices with their start and end apart: 3, of which 3 were waited for; matrix products, arithmetic and copies ran while one was open for 2% of the time, Pallas kernels for 0%

commit v1 on v0

--- a/solution.py
+++ b/solution.py
@@ -2,6 +2,7 @@
 import jax.numpy as jnp
 from jax import lax
 from jax.sharding import PartitionSpec as P
+from jax.lax import axis_index, axis_size, ppermute
 
 BINS = 10
 
@@ -63,7 +64,15 @@
         jnp.zeros((len(row_list), row_width), jnp.float32),
         jnp.zeros((max(len(col_list), 1), column_width), jnp.float32),
     )
-    left_genes = lax.all_gather(expression, "col", axis=0, tiled=True)
+    cores_n = axis_size("col")
+    log = [(tick, (tick + 1) % cores_n) for tick in range(cores_n)]
+    upper = [None] * cores_n
+    upper[cores_n - 1] = expression
+    for pp in range(cores_n - 2, -1, -1):
+        upper[pp] = ppermute(upper[pp + 1], axis_name="col", perm=log)
+    v_next = jnp.concatenate(upper, axis=0)
+    field_out = (axis_index("col") + 1) * expression.shape[0]
+    left_genes = jnp.roll(v_next, shift=field_out, axis=0)
     row_totals, column_totals = block_sums(
         left_genes,
         lax.all_gather(expression, "row", axis=0, tiled=True),

time: 202 us -> 173 us (0.86)
  waiting for transfers between devices: 77.6 us -> 46.9 us
  starting transfers between devices: 0.11 us -> 3.19 us
  other arithmetic: 10.3 us -> 7.89 us
    all_gather x1 -> x0, waiting for transfers between devices: 30.9 us -> none  [on_device(): left_genes = lax.all_gather(expression, 'col', axis=0, tiled=True)]
    ppermute x0 -> x3, waiting for transfers between devices: none -> 25.6 us  [on_device(): upper[pp] = ppermute(upper[pp + 1], axis_name='col', perm=log)]
    all_gather x1, waiting for transfers between devices: 26 us -> 1.29 us  [on_device(): lax.all_gather(expression, 'row', axis=0, tiled=True)]
    ppermute x0 -> x3, starting transfers between devices: none -> 3.11 us  [on_device(): upper[pp] = ppermute(upper[pp + 1], axis_name='col', perm=log)]
  transfers between devices with their start and end apart: 3 -> 5, of which waited for: 3 -> 5; matrix products, arithmetic and copies ran while one was open for 2% -> 1% of each run, Pallas kernels for 0% -> 0%
where the time goes in v1:
time: 173 us
  blocking collectives  79.3 us (46%)
  waiting for transfers between devices  46.9 us (27%)
  matrix products  17.6 us (10%)
  between operations  14.2 us (8%)
  other arithmetic  7.89 us (5%)
  local copies, waits for them, and re-layouts  3.6 us (2%)
  starting transfers between devices  3.19 us (2%)
    psum x1, blocking collectives, on_device(): lax.psum((jnp.sum(weights, axis=1), jnp.sum(degree, axis=1)), ('row', 'co...  40.9 us
    pmax x1, blocking collectives, on_device(): peak = lax.pmax(jnp.max(degree, axis=1), ('row', 'col'))  38.4 us
    ppermute x3, waiting for transfers between devices, on_device(): upper[pp] = ppermute(upper[pp + 1], axis_name='col', perm=log)  25.6 us
    reduce_scatter x1, waiting for transfers between devices, on_device(): lax.psum_scatter(row_totals, 'col', scatter_dimension=1, tiled=True)  19.3 us
    dot_general x2, matrix products, one_block(): lax.dot_general(row_block, right_genes, (((1,), (1,)), ((), ())), preferr...  17.6 us
  transfers between devices with their start and end apart: 5, of which 5 were waited for; matrix products, arithmetic and copies ran while one was open for 1% of the time, Pallas kernels for 0%

profile of v1, /device:TPU:0, one launch (start us, length us, event | category | flops | bytes accessed | tf_op | source)
XLA Modules:
  0.0 172.7 jit_solution(12598485530744555915)
XLA Ops:
  7.2 0.0 copy-start.1
  7.2 0.0 all-gather.2.cloned.1.call-start
  7.2 0.7 all-gather.2.cloned.1.call-update
  7.9 0.0 reduce-scatter.2.cloned.1.call-start
  8.0 3.1 %collective-permute-start = (bf16[128,1024]{1,0:T(8,128)(2,1)}, bf16[128,1024]{1,0:T(8,128)(2,1)S(1)}, u32[]{:S(2)}, u32[]{:S(2)}) collective-permute-start(bf16[128,1024]{1,0:T(8,128)(2,1)} %param.4), channel_id=1, source_target_pairs={{0,1},{1,2},{2,3},{3,0},{4,5},{5,6},{6,7},{7,4},{8,9},{9,10},{10,1... | collective-permute-start | bytes 786440 | tf_op jit(solution)/shard_map/ppermute | solution.py:72
  11.1 8.5 %collective-permute-done = bf16[128,1024]{1,0:T(8,128)(2,1)S(1)} collective-permute-done((bf16[128,1024]{1,0:T(8,128)(2,1)}, bf16[128,1024]{1,0:T(8,128)(2,1)S(1)}, u32[]{:S(2)}, u32[]{:S(2)}) %collective-permute-start) | collective-permute-done | bytes 262176 | tf_op jit(solution)/shard_map/ppermute | solution.py:72
  19.6 0.0 collective-permute-start.1
  19.6 9.3 %collective-permute-done.1 = bf16[128,1024]{1,0:T(8,128)(2,1)S(1)} collective-permute-done((bf16[128,1024]{1,0:T(8,128)(2,1)S(1)}, bf16[128,1024]{1,0:T(8,128)(2,1)S(1)}, u32[]{:S(2)}, u32[]{:S(2)}) %collective-permute-start.1) | collective-permute-done | bytes 262176 | tf_op jit(solution)/shard_map/ppermute | solution.py:72
  28.9 0.0 collective-permute-start.2
  28.9 0.7 convert_element_type.9
  29.5 7.8 %collective-permute-done.2 = bf16[128,1024]{1,0:T(8,128)(2,1)S(1)} collective-permute-done((bf16[128,1024]{1,0:T(8,128)(2,1)S(1)}, bf16[128,1024]{1,0:T(8,128)(2,1)S(1)}, u32[]{:S(2)}, u32[]{:S(2)}) %collective-permute-start.2) | collective-permute-done | bytes 262176 | tf_op jit(solution)/shard_map/ppermute | solution.py:72
  37.4 1.0 constant_dynamic-update-slice_fusion.4
  38.4 0.0 copy-done.1
  38.5 0.2 convert_reduce_fusion.1
  38.7 0.4 fusion.10
  39.1 1.3 all-gather.2.cloned.1.call-done
  40.4 0.0 copy-start
  40.4 2.1 %convert_reduce_fusion = f32[1024]{0:T(1024)S(1)} fusion(bf16[1024,1024]{1,0:T(8,128)(2,1)} %all-gather.2.cloned.1.call-done), kind=kLoop, calls=%fused_computation.20 | loop fusion | flops 2096128 | bytes 2101248 | tf_op jit(solution)/shard_map/reduce_sum | solution.py:12
  42.5 0.1 copy-done
  42.6 0.7 fusion.8
  43.3 19.4 %while.13 = (s32[]{:T(128)}, f32[10,512]{1,0:T(8,128)S(1)}, f32[10]{0:T(128)S(1)}, bf16[512,1024]{1,0:T(8,128)(2,1)S(1)}, bf16[1024,1024]{1,0:T(8,128)(2,1)S(1)}...) while((s32[]{:T(128)}, f32[10,512]{1,0:T(8,128)S(1)}, ...), condition=%wide.region_15.16_spmd, body=%wide.region_4.15_spmd.sunk | while | flops 543686656 | bytes 2715955 | solution.py:52
  43.4 0.1 dynamic_slice.46
  43.4 0.1 dynamic_slice.47
  43.5 0.7 fusion.20
  44.2 8.8 %exponential_reduce_fusion.11 = (f32[256]{0:T(256)S(1)}, f32[256]{0:T(256)S(1)}, f32[256]{0:T(256)S(1)}, f32[256]{0:T(256)S(1)}, f32[256]{0:T(256)S(1)}, /*index...) fusion(f32[]{:T(128)} %bitcast.43, f32[]{:T(128)} %bitcast.44, ...), kind=kOutput, calls=%fused_computation.6.clone.1 | convolution fusion | flops 543684096 | bytes 2641964 | tf_op jit(solution)/shard_map/while/body/eval_jaxpr/dot_general | solution.py:36
  53.0 0.1 stack.78
  53.1 0.1 dynamic_slice.46
  53.1 0.1 dynamic_slice.47
  53.2 0.7 fusion.20
  53.9 8.8 %exponential_reduce_fusion.11 = (f32[256]{0:T(256)S(1)}, f32[256]{0:T(256)S(1)}, f32[256]{0:T(256)S(1)}, f32[256]{0:T(256)S(1)}, f32[256]{0:T(256)S(1)}, /*index...) fusion(f32[]{:T(128)} %bitcast.43, f32[]{:T(128)} %bitcast.44, ...), kind=kOutput, calls=%fused_computation.6.clone.1 | convolution fusion | flops 543684096 | bytes 2641964 | tf_op jit(solution)/shard_map/while/body/eval_jaxpr/dot_general | solution.py:36
  62.7 0.1 stack.78
  62.7 0.0 copy-start.2
  62.8 0.6 copy-done.2
  63.3 0.0 reduce-scatter.2.cloned.1.call-update
  63.4 19.3 %reduce-scatter.2.cloned.1.call-done = f32[10,128]{1,0:T(8,128)} async-done(((f32[10,512]{1,0:T(8,128)}), f32[10,128]{1,0:T(8,128)}) %reduce-scatter.2.cloned.1.call-update) | async-done | bytes 5136 | tf_op jit(solution)/shard_map/reduce_scatter | solution.py:84
  82.7 0.8 fusion.14
  83.5 38.4 %pmax.7 = f32[10]{0:T(128)S(1)} all-reduce(f32[10]{0:T(128)S(1)} %get-tuple-element.170), channel_id=1, replica_groups=mesh['row'=8,'col'=4] {'row','col'}, use_global_device_ids=true, to_apply=%region_18.19 | all-reduce | flops 10 | bytes 80 | tf_op jit(solution)/shard_map/pmax | solution.py:85
  121.9 1.3 add_clamp_fusion
  123.2 0.1 maximum_reduce_fusion
  123.4 40.9 %all-reduce = (f32[10,10]{1,0:T(8,128)S(1)}, f32[10]{0:T(128)S(1)}) all-reduce(f32[10,10]{1,0:T(8,128)S(1)} %maximum_reduce_fusion, f32[10]{0:T(128)S(1)} %get-tuple-element.169), channel_id=1, replica_groups=mesh['row'=8,'col'=4] {'row','col'}, use_global_device_ids=true, to_apply=%region_20.21 | all-reduce | flops 110 | bytes 880 | tf_op jit(solution)/shard_map/psum | solution.py:89
  164.2 0.1 fusion.13
  164.4 0.0 copy-start.3
  164.4 0.2 fusion.12
  164.6 0.5 log_multiply_fusion.3
  165.1 0.2 multiply_reduce_fusion
  165.3 0.5 div.61
  165.8 0.0 copy-done.3
  (17 shorter events, 0.2 us)
Async XLA Ops:
  7.2 31.3 %copy-start.1 = (bf16[128,1024]{1,0:T(8,128)(2,1)S(1)}, bf16[128,1024]{1,0:T(8,128)(2,1)}, u32[]{:S(2)}) copy-start(bf16[128,1024]{1,0:T(8,128)(2,1)} %param.4) | copy-start | bytes 786436
  7.2 33.2 %all-gather.2.cloned.1.call-start = ((), (), s32[]{:S(2)}) async-start(), calls=%async_computation.1 | async-start | bytes 2359296 | tf_op jit(solution)/shard_map/all_gather | solution.py:78
  7.9 74.8 %reduce-scatter.2.cloned.1.call-start = ((), (), s32[]{:S(2)}) async-start(), calls=%async_computation.2 | async-start | bytes 40960 | tf_op jit(solution)/shard_map/reduce_scatter | solution.py:84
  8.0 11.6 %collective-permute-start = (bf16[128,1024]{1,0:T(8,128)(2,1)}, bf16[128,1024]{1,0:T(8,128)(2,1)S(1)}, u32[]{:S(2)}, u32[]{:S(2)}) collective-permute-start(bf16[128,1024]{1,0:T(8,128)(2,1)} %param.4), channel_id=1, source_target_pairs={{0,1},{1,2},{2,3},{3,0},{4,5},{5,6},{6,7},{7,4},{8,9},{9,10},{10,1... | collective-permute-start | bytes 786440 | tf_op jit(solution)/shard_map/ppermute | solution.py:72
  19.6 9.3 %collective-permute-start.1 = (bf16[128,1024]{1,0:T(8,128)(2,1)S(1)}, bf16[128,1024]{1,0:T(8,128)(2,1)S(1)}, u32[]{:S(2)}, u32[]{:S(2)}) collective-permute-start(bf16[128,1024]{1,0:T(8,128)(2,1)S(1)} %collective-permute-done), channel_id=1, source_target_pairs={{0,1},{1,2},{2,3},{3,0},{4,5},{5,6},{6,7},{7,4},{8,9},{9,10},{10,1... | collective-permute-start | bytes 786440 | tf_op jit(solution)/shard_map/ppermute | solution.py:72
  28.9 8.4 %collective-permute-start.2 = (bf16[128,1024]{1,0:T(8,128)(2,1)S(1)}, bf16[128,1024]{1,0:T(8,128)(2,1)S(1)}, u32[]{:S(2)}, u32[]{:S(2)}) collective-permute-start(bf16[128,1024]{1,0:T(8,128)(2,1)S(1)} %collective-permute-done.1), channel_id=1, source_target_pairs={{0,1},{1,2},{2,3},{3,0},{4,5},{5,6},{6,7},{7,4},{8,9},{9,10},{10,1... | collective-permute-start | bytes 786440 | tf_op jit(solution)/shard_map/ppermute | solution.py:72
  40.4 2.2 %copy-start = (bf16[1024,1024]{1,0:T(8,128)(2,1)S(1)}, bf16[1024,1024]{1,0:T(8,128)(2,1)}, u32[]{:S(2)}) copy-start(bf16[1024,1024]{1,0:T(8,128)(2,1)} %all-gather.2.cloned.1.call-done) | copy-start | bytes 6291460
  62.7 0.6 copy-start.2
  164.4 1.5 copy-start.3
Sparse Core Ops, SparseCore 0:
  9.9 30.4 all-gather.1
  63.5 19.1 reduce-scatter.1
